TPU v7x, 32 devices: a whole 2x2x4 slice. The times are simulated.
32 devices in a mesh: dap: 8 (over z, x), cplx: 4 (over y, core).
Axes of the slice: x: 2, y: 2, z: 4, core: 2. Of those that a mesh axis runs over, the one named last changes fastest.
Arguments:
- pair: bfloat16 [96, 384, 128], P('dap', 'cplx'), parts along dimension 1, may hold values from -6 to 6
- cotangent: bfloat16 [96, 384, 128], P('dap', 'cplx'), parts along dimension 1, may hold values from -6 to 6
- residue_mask: int32 [384], P('cplx'), parts along dimension 0, may hold values 0 or 1
- chain_ids: int32 [384], P('cplx'), parts along dimension 0, may hold values from 0 to 2, never falling along the last dimension, each value on 1 to 48 neighbouring positions
- chain_embed: float32 [2, 128], replicated, may hold values from -4 to 4
- out_norm_gain: float32 [128], replicated, may hold values from 0.25 to 1.75
- out_proj: bfloat16 [128, 512], replicated, may hold values from -0.5 to 0.5
- out_gate: bfloat16 [128, 128], replicated, may hold values from -0.5 to 0.5
- out_mid_gain: float32 [128], replicated, may hold values from 0.25 to 1.75
- out_final: bfloat16 [128, 128], replicated, may hold values from -0.5 to 0.5
- in_norm_gain: float32 [128], replicated, may hold values from 0.25 to 1.75
- in_proj: bfloat16 [128, 512], replicated, may hold values from -0.5 to 0.5
- in_gate: bfloat16 [128, 128], replicated, may hold values from -0.5 to 0.5
- in_mid_gain: float32 [128], replicated, may hold values from 0.25 to 1.75
- in_final: bfloat16 [128, 128], replicated, may hold values from -0.5 to 0.5
Outputs:
- pair_grad: bfloat16 [96, 384, 128], P('dap', 'cplx'), parts along dimension 1
- grad_proj: float32 [512, 512], P('cplx'), parts along dimension 0
- grad_gate: float32 [512, 128], P('cplx'), parts along dimension 0
- grad_final: float32 [512, 128], P('cplx'), parts along dimension 0
- grad_norm_gain: float32 [512], P('cplx'), parts along dimension 0
- grad_mid_gain: float32 [512], P('cplx'), parts along dimension 0
There are 4 independent parts, one for each index of `cplx`. A program takes and returns all parts, laid end to end along the dimension named above; an argument that names none is the same for every part. Nothing has to cross between parts.
Inputs may be any that keep to these rules, and one draw needn't show every extreme that they name: `chain_ids`: chain numbers never fall along the residues; each chain has at most 48 residues.
All inputs are finite; a program needn't handle non-finite values.
Results may differ from a plain program's by a relative error of at most 0.019.
Values may be sent and summed in bfloat16 or wider, within the bound.
A program may use at most 128 MiB of HBM per device.

v0:
```python
import jax
import jax.numpy as jnp
from jax import lax
from jax.sharding import PartitionSpec as P


def layer_norm(values_in, gain):
    average = jnp.mean(values_in, axis=-1, keepdims=True)
    centred = values_in - average
    variance = jnp.mean(centred * centred, axis=-1, keepdims=True)
    return centred * lax.rsqrt(variance + 1e-05) * gain


def gated_pair(projected, pair_mask, hidden_width):
    masked = pair_mask[..., None]
    left_act = (
        masked
        * jax.nn.sigmoid(projected[..., :hidden_width])
        * projected[..., hidden_width : 2 * hidden_width]
    )
    right_act = (
        masked
        * jax.nn.sigmoid(projected[..., 2 * hidden_width : 3 * hidden_width])
        * projected[..., 3 * hidden_width :]
    )
    return (left_act, right_act)


def shards(
    pair,
    cotangent,
    residue_mask,
    chain_ids,
    chain_embed,
    out_norm_gain,
    out_proj,
    out_gate,
    out_mid_gain,
    out_final,
    in_norm_gain,
    in_proj,
    in_gate,
    in_mid_gain,
    in_final,
):
    f32 = jnp.float32
    bf16 = jnp.bfloat16
    row_count = pair.shape[0]
    res_count = pair.shape[1]
    hidden_width = out_final.shape[0]
    inv_count = 1.0 / res_count
    row_start = lax.axis_index("dap") * row_count
    row_mask = lax.dynamic_slice_in_dim(residue_mask, row_start, row_count, 0)
    row_chain = lax.dynamic_slice_in_dim(chain_ids, row_start, row_count, 0)
    pair_mask = (row_mask[:, None] * residue_mask[None, :]).astype(f32)
    same_chain = row_chain[:, None] == chain_ids[None, :]
    start = pair.astype(f32) + jnp.where(same_chain[..., None], chain_embed[1], chain_embed[0])
    out_normed = layer_norm(start, out_norm_gain).astype(bf16)
    projected = jnp.dot(out_normed, out_proj, preferred_element_type=f32)
    left_act, right_act = gated_pair(projected, pair_mask, hidden_width)
    left_b = left_act.astype(bf16)
    right_b = right_act.astype(bf16)
    x_out = jnp.einsum(
        "ikc,jkc->ijc",
        left_b,
        lax.all_gather(right_b, "dap", axis=0, tiled=True),
        preferred_element_type=f32,
    )
    y_out = layer_norm(x_out, out_mid_gain).astype(bf16)
    update = jax.nn.sigmoid(jnp.dot(out_normed, out_gate, preferred_element_type=f32)) * jnp.dot(
        y_out, out_final, preferred_element_type=f32
    )
    pair_mid = (start + update).astype(bf16)
    mid_f32 = pair_mid.astype(f32)
    normed_f32, norm_back = jax.vjp(layer_norm, mid_f32, in_norm_gain)
    in_normed = normed_f32.astype(bf16)
    proj_in = jnp.dot(in_normed, in_proj, preferred_element_type=f32)
    (left_in, right_in), glu_back = jax.vjp(
        lambda proj_val: gated_pair(proj_val, pair_mask, hidden_width), proj_in
    )
    left_ib = left_in.astype(bf16)
    right_ib = right_in.astype(bf16)
    columns = lax.all_to_all(left_ib, "dap", split_axis=1, concat_axis=0, tiled=True)
    left_block = columns
    x_in = jnp.einsum(
        "kic,kjc->ijc",
        left_block,
        lax.all_gather(right_ib, "dap", axis=0, tiled=True),
        preferred_element_type=f32,
    )
    y_f32, mid_back = jax.vjp(layer_norm, x_in, in_mid_gain)
    y_in = y_f32.astype(bf16)
    logit = jnp.dot(in_normed, in_gate, preferred_element_type=f32)
    value = jnp.dot(y_in, in_final, preferred_element_type=f32)
    sigma = jax.nn.sigmoid(logit)
    upstream = cotangent.astype(f32)
    grad_value = (upstream * sigma).astype(bf16)
    grad_logit = (upstream * value * sigma * (1.0 - sigma)).astype(bf16)
    grad_final = jnp.einsum("ijc,ijd->cd", y_in, grad_value, preferred_element_type=f32) * inv_count
    grad_gate = (
        jnp.einsum("ijc,ijd->cd", in_normed, grad_logit, preferred_element_type=f32) * inv_count
    )
    grad_y = jnp.dot(grad_value, in_final.T, preferred_element_type=f32)
    grad_x, grad_mid = mid_back(grad_y)
    grad_x_b = grad_x.astype(bf16)
    shard_rows = lax.all_gather(grad_x_b, "dap", axis=0, tiled=True)
    left_block = left_ib
    grad_right = jnp.einsum("kic,ijc->kjc", left_block, shard_rows, preferred_element_type=f32)
    new_block = jnp.einsum("kjc,ijc->kic", right_ib, shard_rows, preferred_element_type=f32)
    grad_p = glu_back((new_block, grad_right))[0].astype(bf16)
    grad_proj = jnp.einsum("ijc,ijd->cd", in_normed, grad_p, preferred_element_type=f32) * inv_count
    grad_normed = jnp.dot(grad_p, in_proj.T, preferred_element_type=f32) + jnp.dot(
        grad_logit, in_gate.T, preferred_element_type=f32
    )
    grad_z, grad_norm = norm_back(grad_normed)
    pair_grad = (upstream + grad_z).astype(bf16)
    reduced = (
        lax.psum(grad_proj.astype(jnp.bfloat16), "dap").astype(jnp.float32),
        lax.psum(grad_gate.astype(jnp.bfloat16), "dap").astype(jnp.float32),
        lax.psum(grad_final.astype(jnp.bfloat16), "dap").astype(jnp.float32),
        lax.psum((grad_norm * inv_count).astype(jnp.bfloat16), "dap").astype(jnp.float32),
        lax.psum((grad_mid * inv_count).astype(jnp.bfloat16), "dap").astype(jnp.float32),
    )
    return (pair_grad, reduced[0], reduced[1], reduced[2], reduced[3], reduced[4])


def solution(mesh):
    placed = (
        P("dap", "cplx", None),
        P("dap", "cplx", None),
        P("cplx"),
        P("cplx"),
        P(),
        P(),
        P(),
        P(),
        P(),
        P(),
        P(),
        P(),
        P(),
        P(),
        P(),
    )
    return jax.shard_map(
        shards,
        mesh=mesh,
        in_specs=placed,
        out_specs=(
            P("dap", "cplx", None),
            P("cplx", None),
            P("cplx", None),
            P("cplx", None),
            P("cplx"),
            P("cplx"),
        ),
        check_vma=False,
    )
```

profile of v0, /device:TPU:0, one launch (start us, length us, event | category | flops | bytes accessed | tf_op | source)
XLA Modules:
  0.0 371.3 jit_solution(1143531026395006253)
XLA Ops:
  7.2 0.7 dynamic_slice.7
  8.0 0.7 broadcast_compare_fusion
  8.7 0.8 slice_bitcast_fusion.1
  9.5 1.4 fusion.41
  10.9 1.6 multiply_reduce_fusion.7
  12.5 0.7 dynamic_slice.6
  13.2 0.7 multiply_convert_fusion.10
  13.9 1.9 fusion.47
  15.9 1.1 fusion.28
  17.0 1.2 copy.47
  18.3 1.7 fusion.8
  19.9 51.8 %all-gather.4.cloned.1.call-done = bf16[96,96,128]{2,1,0:T(8,128)(2,1)} async-done(((bf16[12,96,128]{2,1,0:T(8,128)(2,1)}), bf16[96,96,128]{2,1,0:T(8,128)(2,1)}) %all-gather.4.cloned.1.call-update) | async-done | bytes 2359312 | tf_op jit(solution)/shard_map/all_gather | solution.py:66
  71.7 3.5 copy.46
  75.2 2.8 fusion.62
  81.5 1.4 copy-done.1
  82.9 1.1 multiply_convert_fusion.2
  84.0 0.9 copy.49
  84.9 3.5 all-to-all-start
  88.4 1.1 fusion.5
  89.5 17.3 %all-to-all-done = bf16[12,96,128]{2,0,1:T(8,128)(2,1)S(1)} async-done(((bf16[12,96,128]{2,0,1:T(8,128)(2,1)}), bf16[12,96,128]{2,0,1:T(8,128)(2,1)S(1)}, u32[]{:S(2)}, u32[]{:S(2)}) %all-to-all-start) | async-done | bytes 294944 | tf_op jit(solution)/shard_map/all_to_all | solution.py:83
  107.0 1.2 copy.53
  108.2 29.5 %all-gather.6.cloned.1.call-done = bf16[96,96,128]{2,1,0:T(8,128)(2,1)} async-done(((bf16[12,96,128]{2,1,0:T(8,128)(2,1)}), bf16[96,96,128]{2,1,0:T(8,128)(2,1)}) %all-gather.6.cloned.1.call-update) | async-done | bytes 2359312 | tf_op jit(solution)/shard_map/all_gather | solution.py:88
  137.7 3.5 copy.52
  141.3 3.0 fusion.64
  144.2 1.6 copy.54
  146.9 0.8 multiply_reduce_fusion.1
  147.7 1.5 add_convert_fusion.1
  149.4 1.2 copy.59
  150.6 1.2 copy.56
  153.5 0.9 fusion.16
  154.4 1.3 fusion.17
  155.7 44.1 %all-gather.8.cloned.1.call-done = bf16[96,96,128]{2,1,0:T(8,128)(2,1)} async-done(((bf16[12,96,128]{2,1,0:T(8,128)(2,1)}), bf16[96,96,128]{2,1,0:T(8,128)(2,1)}) %all-gather.8.cloned.1.call-update) | async-done | bytes 2359312 | tf_op jit(solution)/shard_map/all_gather | solution.py:106
  199.8 3.5 copy.55
  203.3 3.8 %fusion.66 = f32[128,96,12]{1,2,0:T(8,128)} fusion(bf16[96,96,128]{1,0,2:T(8,128)(2,1)S(1)} %copy.55, bf16[12,96,128]{1,0,2:T(8,128)(2,1)} %copy.59), kind=kOutput, calls=%fused_computation.126 | convolution fusion | flops 28311552 | bytes 3244032 | tf_op jit(solution)/shard_map/kjc,ijc->kic/dot_general | solution.py:109
  207.1 2.4 copy.60
  209.4 2.9 fusion.65
  212.4 1.5 copy.57
  213.9 2.4 bitcast_multiply_fusion.3
  217.3 1.0 fusion.13
  218.9 0.8 multiply_reduce_fusion.2
  220.8 1.5 fusion.19
  222.3 66.6 %all-reduce.10.cloned.1.call-done = (bf16[128,128]{1,0:T(8,128)(2,1)}, bf16[128,128]{1,0:T(8,128)(2,1)}, bf16[128]{0:T(256)(128)(2,1)}, bf16[128]{0:T(256)(128)(2,1)}) async-done(((bf16[128,128]{1,0:T(8,128)(2,1)}, bf16[128,128]{1,0:T(8,128)(2,1)}, bf16[128]{0:T(256)(128)(2,1)}, bf16[128]{0:T(256)(128)(2,1)}), (bf16[128,128]{1,0:T(8,128)(2,1)}, bf16[128,128]{1,0:T(8,128)(2,1)}, bf16[128]{0:T(256)(128)(2,1)}, ...) | async-done | bytes 66064 | tf_op jit(solution)/shard_map/psum | solution.py:119
  288.9 1.4 convert_element_type.109
  290.3 1.4 convert_element_type.111
  291.7 1.1 convert_element_type.113
  292.8 1.1 convert_element_type.115
  293.9 69.3 %all-reduce.8.cloned.1.call-done = bf16[128,512]{1,0:T(8,128)(2,1)} async-done(((bf16[128,512]{1,0:T(8,128)(2,1)}), bf16[128,512]{1,0:T(8,128)(2,1)}) %all-reduce.8.cloned.1.call-update) | async-done | bytes 131088 | tf_op jit(solution)/shard_map/psum | solution.py:118
  363.2 1.6 convert_element_type.107
  (87 shorter events, 9.3 us)
Async XLA Ops:
  7.2 73.9 %copy-start = (bf16[128,512]{1,0:T(8,128)(2,1)S(1)}, bf16[128,512]{1,0:T(8,128)(2,1)}, u32[]{:S(2)}) copy-start(bf16[128,512]{1,0:T(8,128)(2,1)} %param.26) | copy-start | bytes 393220
  7.2 64.5 %all-gather.4.cloned.1.call-start = ((), (), s32[]{:S(2)}) async-start(), calls=%async_computation.1 | async-start | bytes 2654208 | tf_op jit(solution)/shard_map/all_gather | solution.py:66
  15.9 2.4 copy-start.5
  15.9 2.4 copy-start.23
  15.9 2.4 copy-start.25
  17.0 120.7 %all-gather.6.cloned.1.call-start = ((), (), s32[]{:S(2)}) async-start(), calls=%async_computation.2 | async-start | bytes 2654208 | tf_op jit(solution)/shard_map/all_gather | solution.py:88
  75.2 3.1 copy-start.24
  78.0 1.0 copy-start.6
  78.0 1.2 copy-start.17
  78.0 1.2 copy-start.19
  78.1 2.6 copy-start.22
  79.8 0.8 copy-start.2
  81.1 7.4 %copy-start.14 = (bf16[12,96,128]{2,1,0:T(8,128)(2,1)}, bf16[12,96,128]{2,1,0:T(8,128)(2,1)S(1)}, u32[]{:S(2)}) copy-start(bf16[12,96,128]{2,1,0:T(8,128)(2,1)S(1)} %multiply_convert_fusion.4) | copy-start | bytes 884740
  81.5 1.4 copy-start.1
  82.9 5.5 %copy-start.20 = (bf16[128,128]{1,0:T(8,128)(2,1)S(1)}, bf16[128,128]{1,0:T(8,128)(2,1)}, u32[]{:S(2)}) copy-start(bf16[128,128]{1,0:T(8,128)(2,1)} %param.27) | copy-start | bytes 98308
  84.0 22.9 %copy-start.9 = (bf16[12,96,128]{2,1,0:T(8,128)(2,1)}, bf16[12,96,128]{2,1,0:T(8,128)(2,1)S(1)}, u32[]{:S(2)}) copy-start(bf16[12,96,128]{2,1,0:T(8,128)(2,1)S(1)} %get-tuple-element.22) | copy-start | bytes 884740
  84.9 22.0 %all-to-all-start = ((bf16[12,96,128]{2,0,1:T(8,128)(2,1)}), bf16[12,96,128]{2,0,1:T(8,128)(2,1)S(1)}, u32[]{:S(2)}, u32[]{:S(2)}) async-start(bf16[12,96,128]{2,0,1:T(8,128)(2,1)} %copy.49), calls=%async_computation | async-start | bytes 786432 | tf_op jit(solution)/shard_map/all_to_all | solution.py:83
  88.4 111.4 %all-gather.8.cloned.1.call-start = ((), (), s32[]{:S(2)}) async-start(), calls=%async_computation.3 | async-start | bytes 2654208 | tf_op jit(solution)/shard_map/all_gather | solution.py:106
  141.2 4.9 %copy-start.18 = (bf16[128,128]{1,0:T(8,128)(2,1)S(1)}, bf16[128,128]{1,0:T(8,128)(2,1)}, u32[]{:S(2)}) copy-start(bf16[128,128]{1,0:T(8,128)(2,1)} %param.29) | copy-start | bytes 98308
  141.2 4.9 %copy-start.21 = (f32[128]{0:T(128)S(1)}, f32[128]{0:T(128)}, u32[]{:S(2)}) copy-start(f32[128]{0:T(128)} %param.28) | copy-start | bytes 1540
  144.2 1.9 copy-start.4
  144.2 1.9 copy-start.7
  146.2 3.2 copy-start.11
  146.9 3.7 %copy-start.10 = (bf16[12,96,128]{2,1,0:T(8,128)(2,1)S(1)}, bf16[12,96,128]{2,1,0:T(8,128)(2,1)}, u32[]{:S(2)}) copy-start(bf16[12,96,128]{2,1,0:T(8,128)(2,1)} %copy-done.9) | copy-start | bytes 884740
  147.7 5.9 %copy-start.15 = (bf16[12,96,128]{2,1,0:T(8,128)(2,1)S(1)}, bf16[12,96,128]{2,1,0:T(8,128)(2,1)}, u32[]{:S(2)}) copy-start(bf16[12,96,128]{2,1,0:T(8,128)(2,1)} %copy-done.14) | copy-start | bytes 884740
  149.2 139.7 %all-reduce.10.cloned.1.call-start = ((), (), s32[]{:S(2)}) async-start(), calls=%async_computation.5 | async-start | bytes 133120 | tf_op jit(solution)/shard_map/psum | solution.py:119
  152.8 0.7 copy-start.12
  216.3 1.0 copy-start.16
  217.3 1.1 copy-start.3
  217.3 1.1 copy-start.13
  218.3 2.5 copy-start.8
  220.2 143.0 %all-reduce.8.cloned.1.call-start = ((), (), s32[]{:S(2)}) async-start(), calls=%async_computation.4 | async-start | bytes 262144 | tf_op jit(solution)/shard_map/psum | solution.py:118
Sparse Core Ops, SparseCore 0:
  17.1 54.5 all-gather.3
  84.1 53.5 all-gather.5
  149.3 50.4 all-gather.7
  220.3 68.4 all-reduce.9
  292.6 70.4 all-reduce.7
where the time goes:
time: 372 us; the launch traced here: 371 us
  waiting for transfers between devices  279 us (75%)
  local copies, waits for them, and re-layouts  27.9 us (8%)
  matrix products  23.6 us (6%)
  other arithmetic  22.7 us (6%)
  between operations  14.2 us (4%)
  starting transfers between devices  3.84 us (1%)
    psum x1, waiting for transfers between devices, shards(): lax.psum(grad_proj.astype(jnp.bfloat16), 'dap').astype(jnp.float32)  69.3 us
    psum x1, waiting for transfers between devices, shards(): lax.psum(grad_gate.astype(jnp.bfloat16), 'dap').astype(jnp.float32)  66.6 us
    all_gather x1, waiting for transfers between devices, shards(): lax.all_gather(right_b, 'dap', axis=0, tiled=True)  51.8 us
    all_gather x1, waiting for transfers between devices, shards(): shard_rows = lax.all_gather(grad_x_b, 'dap', axis=0, tiled=True)  44.1 us
    all_gather x1, waiting for transfers between devices, shards(): lax.all_gather(right_ib, 'dap', axis=0, tiled=True)  29.5 us
    all_to_all x1, waiting for transfers between devices, shards(): lax.all_to_all(left_ib, 'dap', split_axis=1, concat_axis=0, tiled=True)  17.3 us
  transfers between devices with their start and end apart: 6, of which 6 were waited for; matrix products, arithmetic and copies ran while one was open for 5% of the time, Pallas kernels for 0%

commit v1 on v0

--- a/solution.py
+++ b/solution.py
@@ -80,7 +80,10 @@
     )
     left_ib = left_in.astype(bf16)
     right_ib = right_in.astype(bf16)
-    columns = lax.all_to_all(left_ib, "dap", split_axis=1, concat_axis=0, tiled=True)
+    columns = jnp.concatenate(
+        lax.all_to_all(jnp.stack(jnp.split(left_ib, lax.axis_size("dap"), axis=1)), "dap", 0, 0),
+        axis=0,
+    )
     left_block = columns
     x_in = jnp.einsum(
         "kic,kjc->ijc",

time: 372 us -> 376 us (1.011)
  local copies, waits for them, and re-layouts: 27.9 us -> 32.3 us
    unnamed x52 -> x59, local copies, waits for them, and re-layouts: 3.78 us -> 8.27 us
  transfers between devices with their start and end apart: 6 -> 6, of which waited for: 6 -> 6; matrix products, arithmetic and copies ran while one was open for 5% -> 6% of each run, Pallas kernels for 0% -> 0%
where the time goes in v1:
time: 376 us; the launch traced here: 375 us
  waiting for transfers between devices  278 us (74%)
  local copies, waits for them, and re-layouts  32.3 us (9%)
  matrix products  23.7 us (6%)
  other arithmetic  22.6 us (6%)
  between operations  14.2 us (4%)
  starting transfers between devices  3.84 us (1%)
    psum x1, waiting for transfers between devices, shards(): lax.psum(grad_proj.astype(jnp.bfloat16), 'dap').astype(jnp.float32)  69.3 us
    psum x1, waiting for transfers between devices, shards(): lax.psum(grad_gate.astype(jnp.bfloat16), 'dap').astype(jnp.float32)  66.6 us
    all_gather x1, waiting for transfers between devices, shards(): lax.all_gather(right_b, 'dap', axis=0, tiled=True)  51.8 us
    all_gather x1, waiting for transfers between devices, shards(): shard_rows = lax.all_gather(grad_x_b, 'dap', axis=0, tiled=True)  43.9 us
    all_gather x1, waiting for transfers between devices, shards(): lax.all_gather(right_ib, 'dap', axis=0, tiled=True)  27.6 us
    all_to_all x1, waiting for transfers between devices, shards(): lax.all_to_all(jnp.stack(jnp.split(left_ib, lax.axis_size('dap'), axis=1)...  18.6 us
    unnamed x59, local copies, waits for them, and re-layouts  8.27 us
  transfers between devices with their start and end apart: 6, of which 6 were waited for; matrix products, arithmetic and copies ran while one was open for 6% of the time, Pallas kernels for 0%

profile of v1, /device:TPU:0, one launch (start us, length us, event | category | flops | bytes accessed | tf_op | source)
XLA Modules:
  0.0 375.1 jit_solution(12373985218139913331)
XLA Ops:
  7.2 0.7 dynamic_slice.7
  8.0 0.7 broadcast_compare_fusion
  8.7 0.8 slice_bitcast_fusion.9
  9.5 1.4 fusion.41
  10.9 1.6 multiply_reduce_fusion.7
  12.5 0.7 dynamic_slice.6
  13.2 0.7 multiply_convert_fusion.10
  13.9 1.9 fusion.47
  15.9 1.1 fusion.28
  17.0 1.2 copy.34
  18.3 1.7 fusion.8
  19.9 51.8 %all-gather.4.cloned.1.call-done = bf16[96,96,128]{2,1,0:T(8,128)(2,1)} async-done(((bf16[12,96,128]{2,1,0:T(8,128)(2,1)}), bf16[96,96,128]{2,1,0:T(8,128)(2,1)}) %all-gather.4.cloned.1.call-update) | async-done | bytes 2359312 | tf_op jit(solution)/shard_map/all_gather | solution.py:66
  71.7 3.5 copy.33
  75.2 2.8 fusion.70
  81.5 1.4 copy-done.1
  83.0 1.1 multiply_convert_fusion.2
  84.0 0.7 fusion.58
  89.1 3.5 all-to-all-start
  92.7 1.2 fusion.5
  93.8 18.6 %all-to-all-done = bf16[8,12,12,128]{3,2,1,0:T(8,128)(2,1)S(1)} async-done(((bf16[8,12,12,128]{3,2,1,0:T(8,128)(2,1)}), bf16[8,12,12,128]{3,2,1,0:T(8,128)(2,1)S(1)}, u32[]{:S(2)}, u32[]{:S(2)}) %all-to-all-start) | async-done | bytes 294944 | tf_op jit(solution)/shard_map/all_to_all | solution.py:84
  112.5 1.4 copy.37
  113.9 27.6 %all-gather.6.cloned.1.call-done = bf16[96,96,128]{2,1,0:T(8,128)(2,1)} async-done(((bf16[12,96,128]{2,1,0:T(8,128)(2,1)}), bf16[96,96,128]{2,1,0:T(8,128)(2,1)}) %all-gather.6.cloned.1.call-update) | async-done | bytes 2359312 | tf_op jit(solution)/shard_map/all_gather | solution.py:91
  141.5 3.5 copy.36
  145.1 3.0 fusion.72
  148.0 1.6 copy.38
  150.7 0.8 multiply_reduce_fusion.1
  151.5 1.4 add_convert_fusion.1
  153.2 1.2 copy.43
  154.4 1.2 copy.40
  157.4 0.9 fusion.16
  158.3 1.3 fusion.17
  159.6 43.9 %all-gather.8.cloned.1.call-done = bf16[96,96,128]{2,1,0:T(8,128)(2,1)} async-done(((bf16[12,96,128]{2,1,0:T(8,128)(2,1)}), bf16[96,96,128]{2,1,0:T(8,128)(2,1)}) %all-gather.8.cloned.1.call-update) | async-done | bytes 2359312 | tf_op jit(solution)/shard_map/all_gather | solution.py:109
  203.5 3.5 copy.39
  207.0 3.8 %fusion.74 = f32[128,96,12]{1,2,0:T(8,128)} fusion(bf16[96,96,128]{1,0,2:T(8,128)(2,1)S(1)} %copy.39, bf16[12,96,128]{1,0,2:T(8,128)(2,1)} %copy.43), kind=kOutput, calls=%fused_computation.142 | convolution fusion | flops 28311552 | bytes 3244032 | tf_op jit(solution)/shard_map/kjc,ijc->kic/dot_general | solution.py:112
  210.8 2.4 copy.44
  213.2 3.0 fusion.73
  216.1 1.5 copy.41
  217.7 2.4 bitcast_multiply_fusion.3
  221.0 1.0 fusion.13
  222.7 0.8 multiply_reduce_fusion.2
  224.6 1.5 fusion.19
  226.0 66.6 %all-reduce.10.cloned.1.call-done = (bf16[128,128]{1,0:T(8,128)(2,1)}, bf16[128,128]{1,0:T(8,128)(2,1)}, bf16[128]{0:T(256)(128)(2,1)}, bf16[128]{0:T(256)(128)(2,1)}) async-done(((bf16[128,128]{1,0:T(8,128)(2,1)}, bf16[128,128]{1,0:T(8,128)(2,1)}, bf16[128]{0:T(256)(128)(2,1)}, bf16[128]{0:T(256)(128)(2,1)}), (bf16[128,128]{1,0:T(8,128)(2,1)}, bf16[128,128]{1,0:T(8,128)(2,1)}, bf16[128]{0:T(256)(128)(2,1)}, ...) | async-done | bytes 66064 | tf_op jit(solution)/shard_map/psum | solution.py:122
  292.6 1.4 convert_element_type.109
  294.0 1.4 convert_element_type.111
  295.4 1.1 convert_element_type.113
  296.5 1.1 convert_element_type.115
  297.6 69.3 %all-reduce.8.cloned.1.call-done = bf16[128,512]{1,0:T(8,128)(2,1)} async-done(((bf16[128,512]{1,0:T(8,128)(2,1)}), bf16[128,512]{1,0:T(8,128)(2,1)}) %all-reduce.8.cloned.1.call-update) | async-done | bytes 131088 | tf_op jit(solution)/shard_map/psum | solution.py:121
  366.9 1.6 convert_element_type.107
  (92 shorter events, 13.6 us)
Async XLA Ops:
  7.2 73.9 %copy-start = (bf16[128,512]{1,0:T(8,128)(2,1)S(1)}, bf16[128,512]{1,0:T(8,128)(2,1)}, u32[]{:S(2)}) copy-start(bf16[128,512]{1,0:T(8,128)(2,1)} %param.26) | copy-start | bytes 393220
  7.2 64.5 %all-gather.4.cloned.1.call-start = ((), (), s32[]{:S(2)}) async-start(), calls=%async_computation.1 | async-start | bytes 2654208 | tf_op jit(solution)/shard_map/all_gather | solution.py:66
  15.9 2.4 copy-start.5
  15.9 2.4 copy-start.23
  15.9 2.4 copy-start.25
  17.0 124.5 %all-gather.6.cloned.1.call-start = ((), (), s32[]{:S(2)}) async-start(), calls=%async_computation.2 | async-start | bytes 2654208 | tf_op jit(solution)/shard_map/all_gather | solution.py:91
  75.2 3.1 copy-start.24
  78.0 1.0 copy-start.6
  78.0 1.2 copy-start.17
  78.0 1.2 copy-start.19
  78.1 2.6 copy-start.22
  79.8 0.8 copy-start.2
  81.1 11.6 %copy-start.14 = (bf16[12,96,128]{2,1,0:T(8,128)(2,1)}, bf16[12,96,128]{2,1,0:T(8,128)(2,1)S(1)}, u32[]{:S(2)}) copy-start(bf16[12,96,128]{2,1,0:T(8,128)(2,1)S(1)} %multiply_convert_fusion.4) | copy-start | bytes 884740
  81.5 1.4 copy-start.1
  82.9 9.7 %copy-start.20 = (bf16[128,128]{1,0:T(8,128)(2,1)S(1)}, bf16[128,128]{1,0:T(8,128)(2,1)}, u32[]{:S(2)}) copy-start(bf16[128,128]{1,0:T(8,128)(2,1)} %param.27) | copy-start | bytes 98308
  84.0 29.9 %copy-start.9 = (bf16[12,96,128]{2,1,0:T(8,128)(2,1)}, bf16[12,96,128]{2,1,0:T(8,128)(2,1)S(1)}, u32[]{:S(2)}) copy-start(bf16[12,96,128]{2,1,0:T(8,128)(2,1)S(1)} %get-tuple-element.22) | copy-start | bytes 884740
  89.1 23.3 %all-to-all-start = ((bf16[8,12,12,128]{3,2,1,0:T(8,128)(2,1)}), bf16[8,12,12,128]{3,2,1,0:T(8,128)(2,1)S(1)}, u32[]{:S(2)}, u32[]{:S(2)}) async-start(bf16[8,12,12,128]{3,2,1,0:T(8,128)(2,1)} %fusion.51), calls=%async_computation | async-start | bytes 786432 | tf_op jit(solution)/shard_map/all_to_all | solution.py:84
  92.6 110.9 %all-gather.8.cloned.1.call-start = ((), (), s32[]{:S(2)}) async-start(), calls=%async_computation.3 | async-start | bytes 2654208 | tf_op jit(solution)/shard_map/all_gather | solution.py:109
  145.0 4.9 %copy-start.18 = (bf16[128,128]{1,0:T(8,128)(2,1)S(1)}, bf16[128,128]{1,0:T(8,128)(2,1)}, u32[]{:S(2)}) copy-start(bf16[128,128]{1,0:T(8,128)(2,1)} %param.29) | copy-start | bytes 98308
  145.1 4.9 %copy-start.21 = (f32[128]{0:T(128)S(1)}, f32[128]{0:T(128)}, u32[]{:S(2)}) copy-start(f32[128]{0:T(128)} %param.28) | copy-start | bytes 1540
  148.0 1.9 copy-start.4
  148.0 1.9 copy-start.7
  150.0 3.2 copy-start.11
  150.7 3.7 copy-start.10
  151.5 5.9 %copy-start.15 = (bf16[12,96,128]{2,1,0:T(8,128)(2,1)S(1)}, bf16[12,96,128]{2,1,0:T(8,128)(2,1)}, u32[]{:S(2)}) copy-start(bf16[12,96,128]{2,1,0:T(8,128)(2,1)} %copy-done.14) | copy-start | bytes 884740
  153.0 139.7 %all-reduce.10.cloned.1.call-start = ((), (), s32[]{:S(2)}) async-start(), calls=%async_computation.5 | async-start | bytes 133120 | tf_op jit(solution)/shard_map/psum | solution.py:122
  156.7 0.7 copy-start.12
  220.0 1.0 copy-start.16
  221.0 1.1 copy-start.3
  221.0 1.1 copy-start.13
  222.1 2.5 copy-start.8
  224.0 143.0 %all-reduce.8.cloned.1.call-start = ((), (), s32[]{:S(2)}) async-start(), calls=%async_computation.4 | async-start | bytes 262144 | tf_op jit(solution)/shard_map/psum | solution.py:121
Sparse Core Ops, SparseCore 0:
  17.1 54.5 all-gather.3
  84.2 57.2 all-gather.5
  153.1 50.3 all-gather.7
  224.1 68.4 all-reduce.9
  296.4 70.4 all-reduce.7
